TPU v7x, 32 devices: a whole 2x2x4 slice. The times are simulated.
32 devices in a mesh: row: 4 (over y, core), col: 8 (over z, x).
Axes of the slice: x: 2, y: 2, z: 4, core: 2. Of those that a mesh axis runs over, the one named last changes fastest.
Arguments:
- hidden_acts: bfloat16 [256, 29568], P('row', 'col'), may hold values from -6 to 6
- output_errors: bfloat16 [256, 4096], P('col', 'row'), may hold values from -6 to 6
- col_points: int32 [8], replicated, may hold values from 0 to 16, as said below
- row_points: int32 [4], replicated, may hold values from 0 to 8, as said below
- worker_mask: int32 [4, 8], replicated, may hold values from 0 to 1, as said below
Outputs:
- clipped_grad: float32 [2, 2048, 29568], P(None, 'col', 'row')
Inputs may be any that keep to these rules, and one draw needn't show every extreme that they name: `col_points`: distinct node indices. `row_points`: distinct node indices. `worker_mask`: each row of the grid has between 1 and 2 erased workers.
All inputs are finite; a program needn't handle non-finite values.
Results may differ from a plain program's by a relative error of at most 0.02.
Values may be sent and summed in bfloat16 or wider, within the bound.
A program may use at most 192 MiB of HBM per device.

v0:
```python
import jax
import jax.numpy as jnp
from jax import lax
from jax.sharding import PartitionSpec as P

D = 4096
FF = 29568


def node_value(index, count):
    return jnp.cos(jnp.pi * (2.0 * index.astype(jnp.float32) + 1.0) / (2.0 * count))


def berrut(nodes, signs, live, targets):
    terms = (live * signs)[:, None] / (targets[None, :] - nodes[:, None])
    return terms / jnp.sum(terms, axis=0, keepdims=True)


def rank_signs(points, live):
    lower = (points[None, :] < points[:, None]).astype(jnp.int32)
    ranks = jnp.sum(lower * live[None, :], axis=1)
    return (1 - 2 * (ranks % 2)).astype(jnp.float32)


def encode_blocks(source, weights, block_count, block_width):

    def add_block(index, total):
        piece = lax.dynamic_slice_in_dim(source, index * block_width, block_width, 1).astype(
            jnp.float32
        )
        factor = lax.dynamic_slice_in_dim(weights, index, 1, 0)
        return total + factor * piece

    start = jnp.zeros((source.shape[0], block_width), jnp.float32)
    return lax.fori_loop(0, block_count, add_block, start).astype(jnp.bfloat16)


def shards(hidden_acts, output_errors, col_points, row_points, worker_mask):
    col_count = lax.axis_size("col")
    row_count = lax.axis_size("row")
    col_place = lax.axis_index("col")
    row_place = lax.axis_index("row")
    act_blocks = col_count // 2
    err_blocks = row_count // 2
    act_width = FF // act_blocks
    err_width = D // err_blocks
    data_acts = node_value(jnp.arange(act_blocks), act_blocks)
    data_errs = node_value(jnp.arange(err_blocks), err_blocks)
    work_acts = node_value(col_points, 2 * col_count + 1)
    work_errs = node_value(row_points, 2 * row_count + 1)
    alt_acts = (1 - 2 * (jnp.arange(act_blocks) % 2)).astype(jnp.float32)
    alt_errs = (1 - 2 * (jnp.arange(err_blocks) % 2)).astype(jnp.float32)
    full_acts = lax.all_gather(hidden_acts, "col", axis=1, tiled=True)
    own_node = lax.dynamic_slice_in_dim(work_acts, col_place, 1, 0)
    encode_own = berrut(data_acts, alt_acts, jnp.ones((act_blocks,), jnp.float32), own_node)[:, 0]
    coded_acts = encode_blocks(full_acts, encode_own, act_blocks, act_width)
    full_errs = lax.all_gather(output_errors, "row", axis=1, tiled=True)
    own_err = lax.dynamic_slice_in_dim(work_errs, row_place, 1, 0)
    encode_err = berrut(data_errs, alt_errs, jnp.ones((err_blocks,), jnp.float32), own_err)[:, 0]
    coded_errs = encode_blocks(full_errs, encode_err, err_blocks, err_width)
    all_errs = lax.all_gather(coded_errs, "col", axis=0, tiled=True)
    product = lax.dot_general(
        all_errs,
        lax.all_gather(coded_acts, "row", axis=0, tiled=True),
        (((0,), (0,)), ((), ())),
        preferred_element_type=jnp.float32,
    ).astype(jnp.bfloat16)
    live = lax.dynamic_slice_in_dim(worker_mask, row_place, 1, 0)[0]
    decode_acts = berrut(
        work_acts, rank_signs(col_points, live), live.astype(jnp.float32), data_acts
    )
    decoded = jnp.einsum(
        "jk,jrf->rkf",
        decode_acts,
        lax.all_to_all(product[None], "col", split_axis=1, concat_axis=0, tiled=True).astype(
            jnp.float32
        ),
    ).astype(jnp.bfloat16)
    decoded = decoded.reshape(decoded.shape[0], FF)
    all_rows = jnp.ones((row_count,), jnp.int32)
    decode_errs = berrut(
        work_errs, rank_signs(row_points, all_rows), jnp.ones((row_count,), jnp.float32), data_errs
    )
    grad = jnp.einsum(
        "il,irf->lrf",
        decode_errs,
        lax.all_to_all(decoded[None], "row", split_axis=2, concat_axis=0, tiled=True).astype(
            jnp.float32
        ),
    )
    squares = lax.psum(jnp.sum(grad * grad), ("row", "col"))
    factor = jnp.minimum(1.0, jnp.sqrt(jnp.float32(FF * D)) / jnp.sqrt(squares + 1e-06))
    return grad * factor


def solution(mesh):
    return jax.shard_map(
        shards,
        mesh=mesh,
        in_specs=(P("row", "col"), P("col", "row"), P(), P(), P()),
        out_specs=P(None, "col", "row"),
        check_vma=False,
    )
```

profile of v0, /device:TPU:12, one launch (start us, length us, event | category | flops | bytes accessed | tf_op | source)
XLA Modules:
  0.0 2220.5 jit_solution(384368010853941417)
XLA Ops:
  6.5 0.7 all-gather.9.cloned.1.call-update
  7.3 0.7 multiply_cosine_fusion.2
  8.0 0.6 dynamic_slice.37
  8.7 1.3 divide_reduce_fusion.1
  10.0 6.0 all_gather.12
  15.9 1.3 multiply_divide_fusion.1
  17.2 2.7 while.28
  17.9 0.7 select_add_fusion.4
  19.2 0.7 select_add_fusion.4
  20.0 0.7 convert_element_type.111
  20.7 0.7 dynamic-slice_bitcast_fusion
  21.4 0.9 select_reduce_fusion
  22.3 0.7 fusion.27
  23.6 1.4 divide_reduce_fusion
  25.0 1.3 multiply_divide_fusion
  26.3 52.1 %all-gather.9.cloned.1.call-done = bf16[8,3696,64]{1,2,0:T(8,128)(2,1)} async-done(((bf16[1,3696,64]{1,2,0:T(8,128)(2,1)}), bf16[8,3696,64]{1,2,0:T(8,128)(2,1)}) %all-gather.9.cloned.1.call-update) | async-done | bytes 3784720 | tf_op jit(solution)/shard_map/all_gather | solution.py:53
  78.4 6.1 copy.25
  84.5 6.5 reshape.100
  90.9 12.4 while.29
  91.5 2.5 select_add_fusion.5
  94.6 2.5 select_add_fusion.5
  97.7 2.5 select_add_fusion.5
  100.8 2.5 select_add_fusion.5
  103.3 1.0 convert_element_type.115
  104.4 14.1 all-gather.5.cloned.1.call-done
  118.5 32.8 %all-gather.7.cloned.1.call-done = bf16[256,7392]{1,0:T(8,128)(2,1)} async-done(((bf16[64,7392]{1,0:T(8,128)(2,1)}), bf16[256,7392]{1,0:T(8,128)(2,1)}) %all-gather.7.cloned.1.call-update) | async-done | bytes 3784720 | tf_op jit(solution)/shard_map/all_gather | solution.py:64
  151.3 15.0 convert_bitcast_fusion
  166.2 123.4 %copy.26 = bf16[1,2048,7392]{2,0,1:T(2,128)(2,1)} copy(bf16[1,2048,7392]{1,2,0:T(8,128)(2,1)} %convert_bitcast_fusion) | data formatting | bytes 60555264 | tf_op jit(solution)/shard_map/broadcast_in_dim | solution.py:75
  290.1 188.5 %reduce.2 = bf16[2048,7392]{1,0:T(8,128)(2,1)} reduce(bf16[2048,1,7392]{2,1,0:T(2,128)(2,1)} %bitcast.51, bf16[]{:T(256)} %broadcast.331), dimensions={1}, to_apply=%bitcast.30.reduce_sub_computation | reduce | bytes 60555264
  478.6 48.8 %reshape.104 = bf16[8,2,946176]{2,1,0:T(2,128)(2,1)} reshape(bf16[2048,7392]{1,0:T(8,128)(2,1)} %reduce.2) | data formatting | bytes 60555264
  527.4 7.2 all-to-all-start
  534.8 650.3 %all-to-all-done = bf16[8,2,946176]{2,1,0:T(2,128)(2,1)} async-done(((bf16[8,2,946176]{2,1,0:T(2,128)(2,1)}), bf16[8,2,946176]{2,1,0:T(2,128)(2,1)}, u32[]{:S(2)}, u32[]{:S(2)}) %all-to-all-start) | async-done | bytes 30277664 | tf_op jit(solution)/shard_map/all_to_all | solution.py:75
  1185.1 86.2 %reshape.105 = bf16[2048,1,7392]{2,1,0:T(2,128)(2,1)} reshape(bf16[8,2,946176]{2,1,0:T(2,128)(2,1)} %all-to-all-done) | data formatting | bytes 60555264
  1271.3 30.4 %copy.33 = bf16[1,2048,7392]{2,1,0:T(8,128)(2,1)} copy(bf16[1,2048,7392]{2,0,1:T(2,128)(2,1)} %bitcast.52) | data formatting | bytes 60555264
  1301.7 39.8 %copy.32 = bf16[8,256,7392]{1,0,2:T(8,128)(2,1)} copy(bf16[8,256,7392]{2,1,0:T(8,128)(2,1)} %bitcast.53) | data formatting | bytes 60555264 | tf_op jit(solution)/shard_map/all_to_all | solution.py:75
  1341.5 17.5 convert_bitcast_fusion.1
  1358.9 9.0 copy.28
  1367.9 177.1 %copy.42 = bf16[1,256,29568]{1,0,2:T(2,128)(2,1)} copy(bf16[1,256,29568]{1,2,0:T(8,128)(2,1)S(1)} %bitcast.56) | data formatting | bytes 30277632 | tf_op jit(solution)/shard_map/broadcast_in_dim;reshape | solution.py:87
  1545.0 322.2 %reduce.3 = bf16[29568,256]{1,0:T(8,128)(2,1)} reduce(bf16[29568,1,256]{2,1,0:T(2,128)(2,1)} %bitcast.54, bf16[]{:T(256)} %broadcast.331), dimensions={1}, to_apply=%bitcast.44.reduce_sub_computation | reduce | bytes 30277634
  1867.2 12.0 reshape.106
  1879.2 8.4 all-to-all-start.1
  1888.0 163.4 %all-to-all-done.1 = bf16[4,2,946176]{2,1,0:T(2,128)(2,1)} async-done(((bf16[4,2,946176]{2,1,0:T(2,128)(2,1)}), bf16[4,2,946176]{2,1,0:T(2,128)(2,1)}, u32[]{:S(2)}, u32[]{:S(2)}) %all-to-all-start.1) | async-done | bytes 15138848 | tf_op jit(solution)/shard_map/all_to_all | solution.py:87
  2051.4 33.1 %reshape.107 = bf16[29568,1,256]{2,1,0:T(2,128)(2,1)} reshape(bf16[4,2,946176]{2,1,0:T(2,128)(2,1)} %all-to-all-done.1) | data formatting | bytes 30277632
  2084.5 18.8 copy.34
  2103.3 44.4 %multiply_reduce_fusion = (f32[]{:T(128)}, f32[2,256,7392]{1,0,2:T(2,128)}) fusion(bf16[1,256,4,7392]{1,3,2,0:T(8,128)(2,1)} %bitcast.59, f32[2]{0:T(128)S(1)} %fusion.7, f32[4]{0:T(128)S(1)} %copy-done.1, f32[4]{0:T(128)S(1)} %fusion.17, f32[2]{0:T(128)S(1)} %multiply_cosine_fusion.3), kind=kOutput, calls=%fused_computation.6 | convolution fusion | flops 37847064 | bytes 30277684 | tf_op jit(solution)/shard_map/il,irf->lrf/dot_general | solution.py:84
  2147.7 42.6 %psum.7 = f32[]{:T(128)} all-reduce(f32[]{:T(128)} %get-tuple-element.211), channel_id=1, replica_groups=mesh['row'=4,'col'=8] {'row','col'}, use_global_device_ids=true, to_apply=%region_11.12 | all-reduce | flops 1 | bytes 8 | tf_op jit(solution)/shard_map/psum | solution.py:91
  2191.0 10.6 broadcast_multiply_fusion
  2201.6 12.1 copy.31
  (27 shorter events, 5.5 us)
Async XLA Ops:
  6.5 71.9 %all-gather.9.cloned.1.call-start = ((), (), s32[]{:S(2)}) async-start(), calls=%async_computation.4 | async-start | bytes 4276224 | tf_op jit(solution)/shard_map/all_gather | solution.py:53
  7.3 111.2 %all-gather.5.cloned.1.call-start = ((), (), s32[]{:S(2)}) async-start(), calls=%async_computation.2 | async-start | bytes 1179648 | tf_op jit(solution)/shard_map/all_gather | solution.py:61
  8.0 0.7 copy-start
  20.6 130.6 %all-gather.7.cloned.1.call-start = ((), (), s32[]{:S(2)}) async-start(), calls=%async_computation.3 | async-start | bytes 4751360 | tf_op jit(solution)/shard_map/all_gather | solution.py:64
  527.4 657.6 %all-to-all-start = ((bf16[8,2,946176]{2,1,0:T(2,128)(2,1)}), bf16[8,2,946176]{2,1,0:T(2,128)(2,1)}, u32[]{:S(2)}, u32[]{:S(2)}) async-start(bf16[8,2,946176]{2,1,0:T(2,128)(2,1)} %reshape.104), calls=%async_computation | async-start | bytes 60555264 | tf_op jit(solution)/shard_map/all_to_all | solution.py:75
  1879.2 8.5 copy-start.2
  1879.2 8.7 copy-start.1
  1879.2 172.3 %all-to-all-start.1 = ((bf16[4,2,946176]{2,1,0:T(2,128)(2,1)}), bf16[4,2,946176]{2,1,0:T(2,128)(2,1)}, u32[]{:S(2)}, u32[]{:S(2)}) async-start(bf16[4,2,946176]{2,1,0:T(2,128)(2,1)} %reshape.106), calls=%async_computation.1 | async-start | bytes 30277632 | tf_op jit(solution)/shard_map/all_to_all | solution.py:87
Sparse Core Ops, SparseCore 0:
  9.5 68.8 all-gather.8
  80.5 37.9 all-gather.4
  120.1 31.1 all-gather.6
where the time goes:
time: 2230 us; the launch traced here: 2220 us
  waiting for transfers between devices  913 us (41%)
  local copies, waits for them, and re-layouts  609 us (27%)
  other arithmetic  543 us (24%)
  matrix products  76.8 us (3%)
  blocking collectives  48.6 us (2%)
    all_to_all x1, waiting for transfers between devices, shards(): lax.all_to_all(product[None], 'col', split_axis=1, concat_axis=0, tiled=T...  650 us
    unnamed x4, other arithmetic  511 us
    unnamed x14, local copies, waits for them, and re-layouts  236 us
    another operation x1, local copies, waits for them, and re-layouts, shards(): decoded[None]  177 us
    all_to_all x1, waiting for transfers between devices, shards(): lax.all_to_all(decoded[None], 'row', split_axis=2, concat_axis=0, tiled=T...  163 us
    broadcast_in_dim x1, local copies, waits for them, and re-layouts, shards(): product[None]  123 us
    all_gather x1, waiting for transfers between devices, shards(): full_acts = lax.all_gather(hidden_acts, 'col', axis=1, tiled=True)  52.1 us
  transfers between devices with their start and end apart: 5, of which 5 were waited for; matrix products, arithmetic and copies ran while one was open for 2% of the time, Pallas kernels for 0%

commit v1 on v0

--- a/solution.py
+++ b/solution.py
@@ -5,6 +5,13 @@
 
 D = 4096
 FF = 29568
+
+
+def exchange_blocks(x, axis, split, join):
+    count = lax.axis_size(axis)
+    shards = jnp.stack(jnp.split(x, count, axis=split), axis=0)
+    shards = lax.all_to_all(shards, axis, split_axis=0, concat_axis=0)
+    return jnp.concatenate(shards, axis=join)
 
 
 def node_value(index, count):
@@ -70,11 +77,7 @@
         work_acts, rank_signs(col_points, live), live.astype(jnp.float32), data_acts
     )
     decoded = jnp.einsum(
-        "jk,jrf->rkf",
-        decode_acts,
-        lax.all_to_all(product[None], "col", split_axis=1, concat_axis=0, tiled=True).astype(
-            jnp.float32
-        ),
+        "jk,jrf->rkf", decode_acts, exchange_blocks(product[None], "col", 1, 0).astype(jnp.float32)
     ).astype(jnp.bfloat16)
     decoded = decoded.reshape(decoded.shape[0], FF)
     all_rows = jnp.ones((row_count,), jnp.int32)

time: 2230 us -> 1790 us (0.80)
  local copies, waits for them, and re-layouts: 609 us -> 313 us
  other arithmetic: 543 us -> 354 us
  matrix products: 76.8 us -> 120 us
    unnamed x4 -> x3, other arithmetic: 511 us -> 323 us
    unnamed x14 -> x18, local copies, waits for them, and re-layouts: 236 us -> 99.7 us
    broadcast_in_dim x1 -> x0, local copies, waits for them, and re-layouts: 123 us -> none  [shards(): product[None]]
    dot_general x1, matrix products: 17.5 us -> 60.5 us  [shards(): jnp.einsum('jk,jrf->rkf', decode_acts, exchange_blocks(product[None], 'co...]
    all_to_all x1 -> x0, local copies, waits for them, and re-layouts: 39.8 us -> none  [shards(): lax.all_to_all(product[None], 'col', split_axis=1, concat_axis=0, tiled=T...]
where the time goes in v1:
time: 1790 us; the launch traced here: 1780 us
  waiting for transfers between devices  915 us (51%)
  other arithmetic  354 us (20%)
  local copies, waits for them, and re-layouts  313 us (17%)
  matrix products  120 us (7%)
  blocking collectives  48.6 us (3%)
    all_to_all x1, waiting for transfers between devices, exchange_blocks(): shards = lax.all_to_all(shards, axis, split_axis=0, concat_axis=0)  650 us
    unnamed x3, other arithmetic  323 us
    another operation x1, local copies, waits for them, and re-layouts, shards(): decoded[None]  177 us
    all_to_all x1, waiting for transfers between devices, shards(): lax.all_to_all(decoded[None], 'row', split_axis=2, concat_axis=0, tiled=T...  163 us
    unnamed x18, local copies, waits for them, and re-layouts  99.7 us
    dot_general x1, matrix products, shards(): jnp.einsum('jk,jrf->rkf', decode_acts, exchange_blocks(product[None], 'co...  60.5 us
    all_gather x1, waiting for transfers between devices, shards(): full_acts = lax.all_gather(hidden_acts, 'col', axis=1, tiled=True)  53.8 us
    dot_general x1, matrix products, shards(): jnp.einsum('il,irf->lrf', decode_errs, lax.all_to_all(decoded[None], 'row...  44.4 us
  transfers between devices with their start and end apart: 5, of which 5 were waited for; matrix products, arithmetic and copies ran while one was open for 2% of the time, Pallas kernels for 0%

profile of v1, /device:TPU:12, one launch (start us, length us, event | category | flops | bytes accessed | tf_op | source)
XLA Modules:
  0.0 1779.6 jit_solution(11976807938782614702)
XLA Ops:
  6.5 0.7 all-gather.9.cloned.1.call-update
  7.3 0.7 multiply_cosine_fusion.2
  8.0 0.6 dynamic_slice.37
  8.7 1.3 divide_reduce_fusion.1
  9.9 6.0 all_gather.12
  15.9 1.3 multiply_divide_fusion.1
  17.2 2.7 while.28
  17.9 0.7 select_add_fusion.4
  19.2 0.7 select_add_fusion.4
  19.9 0.7 convert_element_type.111
  20.7 0.7 multiply_cosine_fusion.1
  22.0 1.3 divide_reduce_fusion
  23.3 1.3 multiply_divide_fusion
  24.6 53.8 %all-gather.9.cloned.1.call-done = bf16[8,3696,64]{1,2,0:T(8,128)(2,1)} async-done(((bf16[1,3696,64]{1,2,0:T(8,128)(2,1)}), bf16[8,3696,64]{1,2,0:T(8,128)(2,1)}) %all-gather.9.cloned.1.call-update) | async-done | bytes 3784720 | tf_op jit(solution)/shard_map/all_gather | solution.py:60
  78.4 6.1 copy.25
  84.5 6.3 reshape.101
  90.8 12.4 while.29
  91.4 2.5 select_add_fusion.5
  94.5 2.5 select_add_fusion.5
  97.6 2.5 select_add_fusion.5
  100.7 2.5 select_add_fusion.5
  103.2 1.0 convert_element_type.115
  104.2 14.2 all-gather.5.cloned.1.call-done
  118.5 32.8 %all-gather.7.cloned.1.call-done = bf16[256,7392]{1,0:T(8,128)(2,1)} async-done(((bf16[64,7392]{1,0:T(8,128)(2,1)}), bf16[256,7392]{1,0:T(8,128)(2,1)}) %all-gather.7.cloned.1.call-update) | async-done | bytes 3784720 | tf_op jit(solution)/shard_map/all_gather | solution.py:71
  151.2 15.1 convert_bitcast_fusion
  166.3 4.2 fusion.14
  170.5 4.2 fusion.13
  174.7 4.1 fusion.12
  178.8 4.2 fusion.11
  183.0 4.2 fusion.10
  187.2 4.1 fusion.9
  191.3 4.1 fusion.8
  195.4 4.2 fusion.7
  199.6 7.2 all-to-all-start
  207.2 650.0 %all-to-all-done = bf16[8,1,256,7392]{2,3,1,0:T(8,128)(2,1)} async-done(((bf16[8,1,256,7392]{2,3,1,0:T(8,128)(2,1)}), bf16[8,1,256,7392]{2,3,1,0:T(8,128)(2,1)}, u32[]{:S(2)}, u32[]{:S(2)}) %all-to-all-start) | async-done | bytes 30277664 | tf_op jit(solution)/shard_map/all_to_all | solution.py:13
  857.2 60.5 %convert_bitcast_fusion.1 = bf16[256,4,7392]{0,1,2:T(4,128)(2,1)} fusion(bf16[8,256,7392]{1,2,0:T(8,128)(2,1)} %bitcast.15, f32[4]{0:T(128)S(1)} %fusion.15, f32[8]{0:T(128)S(1)} %multiply_cosine_fusion.1, f32[4]{0:T(128)S(1)} %multiply_cosine_fusion, f32[8]{0:T(128)S(1)} %fusion.39), kind=kOutput, calls=%fused_computation.9 | convolution fusion | flops 128680032 | bytes 45416544 | tf_op jit(solution)/shard_map/jk,jrf->rkf/dot_general | solution.py:79
  917.7 9.0 copy.27
  926.7 176.7 %copy.43 = bf16[1,256,29568]{1,0,2:T(2,128)(2,1)} copy(bf16[1,256,29568]{1,2,0:T(8,128)(2,1)S(1)} %bitcast.82) | data formatting | bytes 30277632 | tf_op jit(solution)/shard_map/broadcast_in_dim;reshape | solution.py:90
  1103.8 322.6 %reduce.2 = bf16[29568,256]{1,0:T(8,128)(2,1)} reduce(bf16[29568,1,256]{2,1,0:T(2,128)(2,1)} %bitcast.80, bf16[]{:T(256)} %broadcast.331), dimensions={1}, to_apply=%bitcast.73.reduce_sub_computation | reduce | bytes 30277634
  1426.4 11.8 reshape.104
  1438.3 8.5 all-to-all-start.1
  1447.2 163.4 %all-to-all-done.1 = bf16[4,2,946176]{2,1,0:T(2,128)(2,1)} async-done(((bf16[4,2,946176]{2,1,0:T(2,128)(2,1)}), bf16[4,2,946176]{2,1,0:T(2,128)(2,1)}, u32[]{:S(2)}, u32[]{:S(2)}) %all-to-all-start.1) | async-done | bytes 15138848 | tf_op jit(solution)/shard_map/all_to_all | solution.py:90
  1610.6 33.1 %reshape.105 = bf16[29568,1,256]{2,1,0:T(2,128)(2,1)} reshape(bf16[4,2,946176]{2,1,0:T(2,128)(2,1)} %all-to-all-done.1) | data formatting | bytes 30277632
  1643.7 18.8 %copy.31 = bf16[1,256,29568]{1,2,0:T(8,128)(2,1)} copy(bf16[1,256,29568]{1,0,2:T(2,128)(2,1)} %bitcast.81) | data formatting | bytes 30277632
  1662.5 44.4 %multiply_reduce_fusion = (f32[]{:T(128)}, f32[2,256,7392]{1,0,2:T(2,128)}) fusion(bf16[1,256,4,7392]{1,3,2,0:T(8,128)(2,1)} %bitcast.85, f32[2]{0:T(128)S(1)} %fusion.19, f32[4]{0:T(128)S(1)} %multiply_cosine_fusion.2, f32[4]{0:T(128)S(1)} %fusion.29, f32[2]{0:T(128)S(1)} %multiply_cosine_fusion.3), kind=kOutput, calls=%fused_computation.8 | convolution fusion | flops 37847064 | bytes 30277684 | tf_op jit(solution)/shard_map/il,irf->lrf/dot_general | solution.py:87
  1706.9 42.6 %psum.7 = f32[]{:T(128)} all-reduce(f32[]{:T(128)} %get-tuple-element.211), channel_id=1, replica_groups=mesh['row'=4,'col'=8] {'row','col'}, use_global_device_ids=true, to_apply=%region_11.12 | all-reduce | flops 1 | bytes 8 | tf_op jit(solution)/shard_map/psum | solution.py:94
  1750.2 10.6 broadcast_multiply_fusion
  1760.8 12.1 copy.30
  (30 shorter events, 5.7 us)
Async XLA Ops:
  6.5 71.9 %all-gather.9.cloned.1.call-start = ((), (), s32[]{:S(2)}) async-start(), calls=%async_computation.4 | async-start | bytes 4276224 | tf_op jit(solution)/shard_map/all_gather | solution.py:60
  7.3 111.2 %all-gather.5.cloned.1.call-start = ((), (), s32[]{:S(2)}) async-start(), calls=%async_computation.2 | async-start | bytes 1179648 | tf_op jit(solution)/shard_map/all_gather | solution.py:68
  20.6 130.6 %all-gather.7.cloned.1.call-start = ((), (), s32[]{:S(2)}) async-start(), calls=%async_computation.3 | async-start | bytes 4751360 | tf_op jit(solution)/shard_map/all_gather | solution.py:71
  199.6 7.2 copy-start.1
  199.6 7.2 copy-start
  199.6 657.6 %all-to-all-start = ((bf16[8,1,256,7392]{2,3,1,0:T(8,128)(2,1)}), bf16[8,1,256,7392]{2,3,1,0:T(8,128)(2,1)}, u32[]{:S(2)}, u32[]{:S(2)}) async-start(bf16[8,1,256,7392]{2,3,1,0:T(8,128)(2,1)} %fusion.7), calls=%async_computation | async-start | bytes 60555264 | tf_op jit(solution)/shard_map/all_to_all | solution.py:13
  1438.3 8.5 copy-start.2
  1438.3 172.3 %all-to-all-start.1 = ((bf16[4,2,946176]{2,1,0:T(2,128)(2,1)}), bf16[4,2,946176]{2,1,0:T(2,128)(2,1)}, u32[]{:S(2)}, u32[]{:S(2)}) async-start(bf16[4,2,946176]{2,1,0:T(2,128)(2,1)} %reshape.104), calls=%async_computation.1 | async-start | bytes 30277632 | tf_op jit(solution)/shard_map/all_to_all | solution.py:90
Sparse Core Ops, SparseCore 0:
  9.5 68.8 all-gather.8
  80.5 37.8 all-gather.4
  120.0 31.1 all-gather.6
